TPU v7x, 128 devices: a whole 4x4x4 slice. The times are simulated.
128 devices in a mesh: sub: 16 (over x, z), fdr: 8 (over y, core).
Axes of the slice: x: 4, y: 4, z: 4, core: 2. Of those that a mesh axis runs over, the one named last changes fastest.
Arguments:
- inverse: bfloat16 [4096, 256, 256], P(('sub', 'fdr')), may hold values from -1 to 1
- cost: float32 [4096, 256, 128], P(('sub', 'fdr')), may hold values from -6 to 6
- lower_limit: float32 [4096, 256], P(('sub', 'fdr')), may hold values from -1.5 to -0.5
- upper_limit: float32 [4096, 256], P(('sub', 'fdr')), may hold values from 0.5 to 1.5
- iface_rows: int32 [4096, 6], P(('sub', 'fdr')), may hold values from 0 to 255, as said below
- substation_of: int32 [4096], P(('sub', 'fdr')), may hold values from 0 to 511, as said below
- live_count: int32 [128], P(('sub', 'fdr')), may hold values from 16 to 32
- reserve_weight: float32 [512], P('sub'), may hold values from 0.5 to 4
- reserve_target: float32 [512, 6, 128], P('sub'), may hold values from -6 to 6
Outputs:
- duals: float32 [4096, 6, 128], P(('sub', 'fdr'))
- consensus: float32 [512, 6, 128], P('sub')
- residual_norms: float32 [5, 2], replicated
- setpoints: float32 [4096, 256, 128], P(('sub', 'fdr'))
Inputs may be any that keep to these rules, and one draw needn't show every extreme that they name: `iface_rows`: each feeder's 6 interface rows are distinct. `substation_of`: of one device's 32 slots at most 3 hang from substations of one owner block (substations k * 32 to k * 32 + 31); for each index of fdr some block gets exactly 3 slots from every device with that index. `live_count`: a device's live feeders fill its first slots; the other slots hold unused data.
All inputs are finite; a program needn't handle non-finite values.
Results may differ from a plain program's by a relative error of at most 0.0069.
Values sent between devices are 32-bit elements; how exact they have to be, the bound alone decides.
A program may use at most 128 MiB of HBM per device.

v0:
```python
import functools

import jax
import jax.numpy as jnp
from jax import lax
from jax.sharding import Mesh
from jax.sharding import PartitionSpec as P

ITERS = 5
SUB = ("sub_0", "sub_1")
FDR = ("fdr_0", "fdr_1")
SUB_FDR = ("sub_0", "sub_1", "fdr_0", "fdr_1")


penalty = 2.0


def over_axes(x, axes):
    return functools.reduce(lax.psum, axes, x)


def over_pieces(x, axis):
    pieces = lax.all_gather(x, axis)
    return pieces.sum(axis=0)


def shards(
    inverse,
    cost,
    lower_limit,
    upper_limit,
    iface_rows,
    substation_of,
    live_count,
    reserve_weight,
    reserve_target,
):
    slot_count = inverse.shape[0]
    iface_count = iface_rows.shape[1]
    scenarios = cost.shape[2]
    flat_width = iface_count * scenarios
    sub_count = lax.axis_size(SUB)
    owned_count = reserve_weight.shape[0]
    total_sub = owned_count * sub_count
    sub_index = lax.axis_index(SUB)
    fdr_index = lax.axis_index(FDR)
    active = (jnp.arange(slot_count, dtype=jnp.int32) < live_count[0]).astype(jnp.float32)
    membership = (substation_of[:, None] == jnp.arange(total_sub, dtype=jnp.int32)[None, :]).astype(
        jnp.float32
    ) * active[:, None]
    tallied = over_axes(jnp.sum(membership, axis=0), SUB_FDR)
    flat_target = reserve_target.reshape(owned_count, flat_width)
    first_row = sub_index * owned_count
    dual_mask = (fdr_index == 0).astype(jnp.float32)
    overflow = max(1, slot_count // (2 * sub_count))
    capacity = max(2, slot_count // sub_count + overflow)
    slot_total = sub_count * capacity
    group_of = substation_of // owned_count
    group_hot = (group_of[:, None] == jnp.arange(sub_count, dtype=jnp.int32)[None, :]).astype(
        jnp.int32
    )
    earlier = jnp.cumsum(group_hot, axis=0) - group_hot
    slot_rank = jnp.sum(earlier * group_hot, axis=1)
    position = group_of * capacity + slot_rank
    slot_match = position[:, None] == jnp.arange(slot_total, dtype=jnp.int32)[None, :]
    slot_hot = slot_match.astype(jnp.float32)
    slot_ids = jnp.sum(slot_match.astype(jnp.int32) * (substation_of + 1)[:, None], axis=0) - 1
    arrived_ids = lax.all_to_all(slot_ids, SUB, split_axis=0, concat_axis=0, tiled=True)
    arrived_hot = (
        (arrived_ids - sub_index * owned_count)[:, None]
        == jnp.arange(owned_count, dtype=jnp.int32)[None, :]
    ).astype(jnp.float32)
    own_members = lax.dynamic_slice_in_dim(tallied, first_row, owned_count, 0)
    feeder_index = jnp.arange(slot_count, dtype=jnp.int32)[:, None]
    scaled_dual = jnp.zeros((slot_count, iface_count, scenarios), jnp.float32)
    local_consensus = jnp.zeros((slot_count, iface_count, scenarios), jnp.float32)
    anchor = jnp.zeros((slot_count, inverse.shape[1], scenarios), jnp.float32)
    old_rows = jnp.zeros((owned_count, flat_width), jnp.float32)
    sums_list = []
    for iteration in range(ITERS):
        right_side = (
            (anchor - cost)
            .at[feeder_index, iface_rows]
            .add(penalty * (local_consensus - scaled_dual))
            .astype(jnp.bfloat16)
        )
        primal = jnp.einsum("fkj,fjs->fks", inverse, right_side, preferred_element_type=jnp.float32)
        anchor = jnp.clip(primal, lower_limit[:, :, None], upper_limit[:, :, None])
        boundary = jnp.take_along_axis(primal, iface_rows[:, :, None], axis=1)
        outgoing = ((boundary + scaled_dual) * active[:, None, None]).reshape(
            slot_count, flat_width
        )
        packed = jnp.einsum("fn,fc->nc", slot_hot, outgoing, precision=lax.Precision.HIGHEST)
        arrived = lax.all_to_all(packed, SUB, split_axis=0, concat_axis=0, tiled=True)
        block_sums = jnp.einsum("no,nc->oc", arrived_hot, arrived, precision=lax.Precision.HIGHEST)
        collected = over_pieces(block_sums, FDR)
        new_rows = (collected + reserve_weight[:, None] * flat_target) / (
            own_members + reserve_weight
        )[:, None]
        dual_local = dual_mask * jnp.sum(own_members[:, None] * (new_rows - old_rows) ** 2)
        old_rows = new_rows
        reply = jnp.einsum("no,oc->nc", arrived_hot, new_rows, precision=lax.Precision.HIGHEST)
        returned = lax.all_to_all(reply, SUB, split_axis=0, concat_axis=0, tiled=True)
        local_consensus = jnp.einsum(
            "fn,nc->fc", slot_hot, returned, precision=lax.Precision.HIGHEST
        ).reshape(slot_count, iface_count, scenarios)
        mismatch = boundary - local_consensus
        scaled_dual = (scaled_dual + mismatch) * active[:, None, None]
        primal_local = jnp.sum(active[:, None, None] * mismatch**2)
        sums_list.append(jnp.stack([primal_local, dual_local]))
    stacked = jnp.stack(sums_list)
    stacked = over_axes(stacked, SUB_FDR)
    residual_norms = jnp.sqrt(stacked) * jnp.array([1.0, penalty], jnp.float32)[None, :]
    consensus = old_rows.reshape(owned_count, iface_count, scenarios)
    return (penalty * scaled_dual, consensus, residual_norms, anchor * active[:, None, None])


def solution(mesh):
    torus = Mesh(mesh.devices.reshape(4, 4, 4, 2), ("sub_0", "sub_1", "fdr_0", "fdr_1"))
    placed = (
        P(SUB_FDR, None, None),
        P(SUB_FDR, None, None),
        P(SUB_FDR, None),
        P(SUB_FDR, None),
        P(SUB_FDR, None),
        P(SUB_FDR),
        P(SUB_FDR),
        P(SUB),
        P(SUB, None, None),
    )
    return jax.shard_map(
        shards,
        mesh=torus,
        in_specs=placed,
        out_specs=(P(SUB_FDR, None, None), P(SUB, None, None), P(), P(SUB_FDR, None, None)),
        check_vma=False,
    )
```

profile of v0, /device:TPU:1, one launch (start us, length us, event | category | flops | bytes accessed | tf_op | source)
XLA Modules:
  0.0 498.8 jit_solution(238715857411386526)
XLA Ops:
  2.4 8.4 %all-to-all-start = ((s32[16,3,1]{1,2,0:T(1,128)}), s32[16,3,1]{1,2,0:T(1,128)S(1)}, u32[]{:S(2)}, u32[]{:S(2)}) async-start(s32[16,3,1]{1,2,0:T(1,128)} %bitcast.5), calls=%async_computation | async-start | bytes 16384 | tf_op jit(solution)/shard_map/all_to_all | solution.py:68
  12.2 5.6 %copy.164 = f32[32,256,128]{1,2,0:T(8,128)} copy(f32[32,256,128]{2,1,0:T(8,128)} %param.13) | data formatting | bytes 8388608 | tf_op args[1]
  17.8 4.6 broadcast_subtract_fusion
  23.3 8.6 %psum.56 = f32[512]{0:T(512)S(1)} all-reduce(f32[512]{0:T(512)S(1)} %select_reduce_fusion), channel_id=1, replica_groups=mesh['sub_0'=4,'sub_1'=4,'fdr_0'=4,'fdr_1'=2] {'sub_0'}, use_global_device_ids=true, to_apply=%region_6.8 | all-reduce | flops 512 | bytes 4096 | tf_op jit(solution)/shard_map/psum | solution.py:19
  31.8 8.4 %psum.57 = f32[512]{0:T(512)S(1)} all-reduce(f32[512]{0:T(512)S(1)} %psum.56), channel_id=1, replica_groups=mesh['sub_0'=4,'sub_1'=4,'fdr_0'=4,'fdr_1'=2] {'sub_1'}, use_global_device_ids=true, to_apply=%region_7.9 | all-reduce | flops 512 | bytes 4096 | tf_op jit(solution)/shard_map/psum | solution.py:19
  40.2 8.7 %psum.58 = f32[512]{0:T(512)S(1)} all-reduce(f32[512]{0:T(512)S(1)} %psum.57), channel_id=1, replica_groups=mesh['sub_0'=4,'sub_1'=4,'fdr_0'=4,'fdr_1'=2] {'fdr_0'}, use_global_device_ids=true, to_apply=%region_8.10 | all-reduce | flops 512 | bytes 4096 | tf_op jit(solution)/shard_map/psum | solution.py:19
  48.9 9.4 %psum.59 = f32[512]{0:T(512)S(1)} all-reduce(f32[512]{0:T(512)S(1)} %psum.58), channel_id=1, replica_groups=mesh['sub_0'=4,'sub_1'=4,'fdr_0'=4,'fdr_1'=2] {'fdr_1'}, use_global_device_ids=true, to_apply=%region_9.11 | all-reduce | flops 512 | bytes 4096 | tf_op jit(solution)/shard_map/psum | solution.py:19
  58.7 19.9 %scatter_fusion = f32[32,256,128]{2,1,0:T(8,128)} fusion(f32[32,256,128]{2,1,0:T(8,128)} %broadcast_subtract_fusion, s32[192]{0:T(256)S(1)} %reshape.388, f32[192,128]{1,0:T(8,128)S(1)} %broadcast.477), kind=kCustom, calls=%fused_computation.5 | custom fusion | flops 24576 | bytes 296448 | tf_op jit(solution)/shard_map/scatter-add | solution.py:84
  78.7 9.3 %minimum_subtract_fusion.3 = (f32[32,256,128]{1,2,0:T(8,128)}, f32[32,256,128]{1,2,0:T(8,128)}) fusion(f32[32,256,128]{1,2,0:T(8,128)} %copy.164, f32[32,256]{1,0:T(8,128)S(1)} %copy-done.1, f32[32,256]{1,0:T(8,128)S(1)} %copy-done.2, bf16[32,256,256]{2,1,0:T(8,128)(2,1)} %param.12, f32[32,256,128]{2,1,0:T(8,128)} %scatter_fusion), kind=kOutput, calls=%fused_computation.14 | convolution fusion | flops 541065216 | bytes 21037056 | tf_op jit(solution)/shard_map/fkj,fjs->fks/dot_general | solution.py:87
  88.0 5.6 %copy.155 = f32[32,256,128]{2,1,0:T(8,128)} copy(f32[32,256,128]{1,2,0:T(8,128)} %get-tuple-element.53) | data formatting | bytes 8388608 | tf_op jit(solution)/shard_map/fkj,fjs->fks/dot_general | solution.py:87
  93.6 4.6 gather_fusion
  99.5 3.5 all-to-all-start.1
  104.4 5.6 %all-to-all-done.1 = f32[16,3,768]{2,1,0:T(4,128)S(1)} async-done(((f32[16,3,768]{2,1,0:T(4,128)}), f32[16,3,768]{2,1,0:T(4,128)S(1)}, u32[]{:S(2)}, u32[]{:S(2)}) %all-to-all-start.1) | async-done | bytes 147488 | tf_op jit(solution)/shard_map/all_to_all | solution.py:94
  110.3 15.1 %all-gather = f32[256,768]{1,0:T(8,128)S(1)} all-gather(f32[32,768]{1,0:T(8,128)S(1)} %fusion.48), channel_id=2, replica_groups=mesh['sub_0'=4,'sub_1'=4,'fdr_0'=4,'fdr_1'=2] {'fdr_0','fdr_1'}, dimensions={0}, use_global_device_ids=true | all-gather | bytes 884736 | tf_op jit(solution)/shard_map/all_gather | solution.py:23
  125.9 0.8 copy.162
  126.7 3.7 all-to-all-start.2
  130.4 5.6 %copy.166 = f32[32,256,128]{2,1,0:T(8,128)} copy(f32[32,256,128]{1,2,0:T(8,128)} %get-tuple-element.52) | data formatting | bytes 8388608 | tf_op jit(solution)/shard_map/sub | solution.py:82
  136.0 1.2 all-to-all-done.2
  137.6 20.0 %scatter_fusion.1 = f32[32,256,128]{2,1,0:T(8,128)} fusion(f32[32,256,128]{2,1,0:T(8,128)} %copy.166, s32[192]{0:T(256)S(1)} %reshape.388, f32[192,128]{1,0:T(8,128)S(1)} %reshape.396), kind=kCustom, calls=%fused_computation.6 | custom fusion | flops 24576 | bytes 296448 | tf_op jit(solution)/shard_map/scatter-add | solution.py:84
  157.6 9.4 %minimum_subtract_fusion.2 = (f32[32,256,128]{1,2,0:T(8,128)}, f32[32,256,128]{1,2,0:T(8,128)}) fusion(f32[32,256,128]{1,2,0:T(8,128)} %copy.164, f32[32,256]{1,0:T(8,128)S(1)} %copy-done.1, f32[32,256]{1,0:T(8,128)S(1)} %copy-done.2, bf16[32,256,256]{2,1,0:T(8,128)(2,1)} %param.12, f32[32,256,128]{2,1,0:T(8,128)} %scatter_fusion.1), kind=kOutput, calls=%fused_computation.13 | convolution fusion | flops 541065216 | bytes 21037056 | tf_op jit(solution)/shard_map/fkj,fjs->fks/dot_general | solution.py:87
  167.0 5.6 %copy.169 = f32[32,256,128]{2,1,0:T(8,128)} copy(f32[32,256,128]{1,2,0:T(8,128)} %get-tuple-element.56) | data formatting | bytes 8388608 | tf_op jit(solution)/shard_map/fkj,fjs->fks/dot_general | solution.py:87
  172.5 4.6 gather_fusion.1
  177.7 12.2 %all_to_all.96 = f32[16,3,768]{2,1,0:T(4,128)S(1)} all-to-all(f32[16,3,768]{2,1,0:T(4,128)S(1)} %copy.172), channel_id=1, replica_groups=mesh['sub_0'=4,'sub_1'=4,'fdr_0'=4,'fdr_1'=2] {'sub_0','sub_1'}, dimensions={0} | all-to-all | bytes 294912 | tf_op jit(solution)/shard_map/all_to_all | solution.py:94
  190.3 15.0 %all-gather.1 = f32[256,768]{1,0:T(8,128)S(1)} all-gather(f32[32,768]{1,0:T(8,128)S(1)} %fusion.47), channel_id=3, replica_groups=mesh['sub_0'=4,'sub_1'=4,'fdr_0'=4,'fdr_1'=2] {'fdr_0','fdr_1'}, dimensions={0}, use_global_device_ids=true | all-gather | bytes 884736 | tf_op jit(solution)/shard_map/all_gather | solution.py:23
  205.8 0.8 copy.173
  206.6 3.5 all-to-all-start.4
  210.1 5.6 %copy.177 = f32[32,256,128]{2,1,0:T(8,128)} copy(f32[32,256,128]{1,2,0:T(8,128)} %get-tuple-element.55) | data formatting | bytes 8388608 | tf_op jit(solution)/shard_map/sub | solution.py:82
  215.7 1.4 all-to-all-done.4
  217.5 20.0 %scatter_fusion.2 = f32[32,256,128]{2,1,0:T(8,128)} fusion(f32[32,256,128]{2,1,0:T(8,128)} %copy.177, s32[192]{0:T(256)S(1)} %reshape.388, f32[192,128]{1,0:T(8,128)S(1)} %reshape.402), kind=kCustom, calls=%fused_computation.7 | custom fusion | flops 24576 | bytes 296448 | tf_op jit(solution)/shard_map/scatter-add | solution.py:84
  237.5 9.4 %minimum_subtract_fusion.1 = (f32[32,256,128]{1,2,0:T(8,128)}, f32[32,256,128]{1,2,0:T(8,128)}) fusion(f32[32,256,128]{1,2,0:T(8,128)} %copy.164, f32[32,256]{1,0:T(8,128)S(1)} %copy-done.1, f32[32,256]{1,0:T(8,128)S(1)} %copy-done.2, bf16[32,256,256]{2,1,0:T(8,128)(2,1)} %param.12, f32[32,256,128]{2,1,0:T(8,128)} %scatter_fusion.2), kind=kOutput, calls=%fused_computation.12 | convolution fusion | flops 541065216 | bytes 21037056 | tf_op jit(solution)/shard_map/fkj,fjs->fks/dot_general | solution.py:87
  246.8 5.6 %copy.180 = f32[32,256,128]{2,1,0:T(8,128)} copy(f32[32,256,128]{1,2,0:T(8,128)} %get-tuple-element.59) | data formatting | bytes 8388608 | tf_op jit(solution)/shard_map/fkj,fjs->fks/dot_general | solution.py:87
  252.4 4.6 gather_fusion.2
  257.6 12.2 %all_to_all.97 = f32[16,3,768]{2,1,0:T(4,128)S(1)} all-to-all(f32[16,3,768]{2,1,0:T(4,128)S(1)} %copy.183), channel_id=1, replica_groups=mesh['sub_0'=4,'sub_1'=4,'fdr_0'=4,'fdr_1'=2] {'sub_0','sub_1'}, dimensions={0} | all-to-all | bytes 294912 | tf_op jit(solution)/shard_map/all_to_all | solution.py:94
  270.1 15.3 %all-gather.2 = f32[256,768]{1,0:T(8,128)S(1)} all-gather(f32[32,768]{1,0:T(8,128)S(1)} %fusion.46), channel_id=4, replica_groups=mesh['sub_0'=4,'sub_1'=4,'fdr_0'=4,'fdr_1'=2] {'fdr_0','fdr_1'}, dimensions={0}, use_global_device_ids=true | all-gather | bytes 884736 | tf_op jit(solution)/shard_map/all_gather | solution.py:23
  285.9 0.8 copy.184
  286.7 3.5 all-to-all-start.6
  290.2 5.6 %copy.188 = f32[32,256,128]{2,1,0:T(8,128)} copy(f32[32,256,128]{1,2,0:T(8,128)} %get-tuple-element.58) | data formatting | bytes 8388608 | tf_op jit(solution)/shard_map/sub | solution.py:82
  295.8 1.4 all-to-all-done.6
  297.6 20.0 %scatter_fusion.3 = f32[32,256,128]{2,1,0:T(8,128)} fusion(f32[32,256,128]{2,1,0:T(8,128)} %copy.188, s32[192]{0:T(256)S(1)} %reshape.388, f32[192,128]{1,0:T(8,128)S(1)} %reshape.408), kind=kCustom, calls=%fused_computation.8 | custom fusion | flops 24576 | bytes 296448 | tf_op jit(solution)/shard_map/scatter-add | solution.py:84
  317.6 9.6 %minimum_subtract_fusion = (f32[32,256,128]{1,2,0:T(8,128)}, f32[32,256,128]{1,2,0:T(8,128)}) fusion(f32[32,256,128]{1,2,0:T(8,128)} %copy.164, f32[32,256]{1,0:T(8,128)S(1)} %copy-done.1, f32[32,256]{1,0:T(8,128)S(1)} %copy-done.2, bf16[32,256,256]{2,1,0:T(8,128)(2,1)} %param.12, f32[32,256,128]{2,1,0:T(8,128)} %scatter_fusion.3), kind=kOutput, calls=%fused_computation.11 | convolution fusion | flops 541065216 | bytes 21037056 | tf_op jit(solution)/shard_map/fkj,fjs->fks/dot_general | solution.py:87
  327.1 5.6 %copy.191 = f32[32,256,128]{2,1,0:T(8,128)} copy(f32[32,256,128]{1,2,0:T(8,128)} %get-tuple-element.62) | data formatting | bytes 8388608 | tf_op jit(solution)/shard_map/fkj,fjs->fks/dot_general | solution.py:87
  332.7 4.6 gather_fusion.3
  337.9 12.2 %all_to_all.98 = f32[16,3,768]{2,1,0:T(4,128)S(1)} all-to-all(f32[16,3,768]{2,1,0:T(4,128)S(1)} %copy.194), channel_id=1, replica_groups=mesh['sub_0'=4,'sub_1'=4,'fdr_0'=4,'fdr_1'=2] {'sub_0','sub_1'}, dimensions={0} | all-to-all | bytes 294912 | tf_op jit(solution)/shard_map/all_to_all | solution.py:94
  350.4 15.0 %all-gather.3 = f32[256,768]{1,0:T(8,128)S(1)} all-gather(f32[32,768]{1,0:T(8,128)S(1)} %fusion.45), channel_id=5, replica_groups=mesh['sub_0'=4,'sub_1'=4,'fdr_0'=4,'fdr_1'=2] {'fdr_0','fdr_1'}, dimensions={0}, use_global_device_ids=true | all-gather | bytes 884736 | tf_op jit(solution)/shard_map/all_gather | solution.py:23
  366.0 0.8 copy.195
  366.7 3.8 all-to-all-start.8
  370.5 5.6 %copy.199 = f32[32,256,128]{2,1,0:T(8,128)} copy(f32[32,256,128]{1,2,0:T(8,128)} %get-tuple-element.61) | data formatting | bytes 8388608 | tf_op jit(solution)/shard_map/sub | solution.py:82
  376.1 1.1 all-to-all-done.8
  377.7 20.0 %scatter_fusion.4 = f32[32,256,128]{2,1,0:T(8,128)} fusion(f32[32,256,128]{2,1,0:T(8,128)} %copy.199, s32[192]{0:T(256)S(1)} %reshape.388, f32[192,128]{1,0:T(8,128)S(1)} %reshape.414), kind=kCustom, calls=%fused_computation.9 | custom fusion | flops 24576 | bytes 296448 | tf_op jit(solution)/shard_map/scatter-add | solution.py:84
  397.6 8.4 %minimum_multiply_fusion = (f32[32,256,128]{1,2,0:T(8,128)}, f32[32,256,128]{1,2,0:T(8,128)}) fusion(f32[32]{0:T(128)S(1)} %compare_convert_fusion, f32[32,256]{1,0:T(8,128)S(1)} %copy-done.1, f32[32,256]{1,0:T(8,128)S(1)} %copy-done.2, bf16[32,256,256]{2,1,0:T(8,128)(2,1)} %param.12, f32[32,256,128]{2,1,0:T(8,128)} %scatter_fusion.4), kind=kOutput, calls=%fused_computation.10 | convolution fusion | flops 541065216 | bytes 16842880 | tf_op jit(solution)/shard_map/fkj,fjs->fks/dot_general | solution.py:87
  406.0 5.6 %copy.202 = f32[32,256,128]{2,1,0:T(8,128)} copy(f32[32,256,128]{1,2,0:T(8,128)} %get-tuple-element.64) | data formatting | bytes 8388608 | tf_op jit(solution)/shard_map/fkj,fjs->fks/dot_general | solution.py:87
  411.6 4.6 gather_fusion.4
  416.8 12.2 %all_to_all.99 = f32[16,3,768]{2,1,0:T(4,128)S(1)} all-to-all(f32[16,3,768]{2,1,0:T(4,128)S(1)} %copy.205), channel_id=1, replica_groups=mesh['sub_0'=4,'sub_1'=4,'fdr_0'=4,'fdr_1'=2] {'sub_0','sub_1'}, dimensions={0} | all-to-all | bytes 294912 | tf_op jit(solution)/shard_map/all_to_all | solution.py:94
  429.3 15.0 %all-gather.4 = f32[256,768]{1,0:T(8,128)S(1)} all-gather(f32[32,768]{1,0:T(8,128)S(1)} %fusion.44), channel_id=6, replica_groups=mesh['sub_0'=4,'sub_1'=4,'fdr_0'=4,'fdr_1'=2] {'fdr_0','fdr_1'}, dimensions={0}, use_global_device_ids=true | all-gather | bytes 884736 | tf_op jit(solution)/shard_map/all_gather | solution.py:23
  444.4 0.9 multiply_reduce_fusion
  445.6 0.8 copy.206
  446.4 3.5 all-to-all-start.10
  453.1 3.7 all-to-all-done.10
  456.9 1.6 multiply_reduce_fusion.5
  462.5 7.5 %psum.60 = f32[5,2]{0,1:T(2,128)S(1)} all-reduce(f32[5,2]{0,1:T(2,128)S(1)} %stack.83), channel_id=1, replica_groups=mesh['sub_0'=4,'sub_1'=4,'fdr_0'=4,'fdr_1'=2] {'sub_0'}, use_global_device_ids=true, to_apply=%region_28.30 | all-reduce | flops 10 | bytes 80 | tf_op jit(solution)/shard_map/psum | solution.py:19
  470.0 6.2 %psum.61 = f32[5,2]{0,1:T(2,128)S(1)} all-reduce(f32[5,2]{0,1:T(2,128)S(1)} %psum.60), channel_id=1, replica_groups=mesh['sub_0'=4,'sub_1'=4,'fdr_0'=4,'fdr_1'=2] {'sub_1'}, use_global_device_ids=true, to_apply=%region_29.31 | all-reduce | flops 10 | bytes 80 | tf_op jit(solution)/shard_map/psum | solution.py:19
  476.2 5.6 %copy.214 = f32[32,256,128]{2,1,0:T(8,128)} copy(f32[32,256,128]{1,2,0:T(8,128)} %get-tuple-element.63) | data formatting | bytes 8388608
  481.8 6.1 %psum.62 = f32[5,2]{0,1:T(2,128)S(1)} all-reduce(f32[5,2]{0,1:T(2,128)S(1)} %psum.61), channel_id=1, replica_groups=mesh['sub_0'=4,'sub_1'=4,'fdr_0'=4,'fdr_1'=2] {'fdr_0'}, use_global_device_ids=true, to_apply=%region_30.32 | all-reduce | flops 10 | bytes 80 | tf_op jit(solution)/shard_map/psum | solution.py:19
  488.6 9.6 %psum.63 = f32[5,2]{0,1:T(2,128)S(1)} all-reduce(f32[5,2]{0,1:T(2,128)S(1)} %psum.62), channel_id=1, replica_groups=mesh['sub_0'=4,'sub_1'=4,'fdr_0'=4,'fdr_1'=2] {'fdr_1'}, use_global_device_ids=true, to_apply=%region_31.33 | all-reduce | flops 10 | bytes 80 | tf_op jit(solution)/shard_map/psum | solution.py:19
  (130 shorter events, 19.7 us)
Async XLA Ops:
  2.4 97.1 %all-to-all-start = ((s32[16,3,1]{1,2,0:T(1,128)}), s32[16,3,1]{1,2,0:T(1,128)S(1)}, u32[]{:S(2)}, u32[]{:S(2)}) async-start(s32[16,3,1]{1,2,0:T(1,128)} %bitcast.5), calls=%async_computation | async-start | bytes 16384 | tf_op jit(solution)/shard_map/all_to_all | solution.py:68
  17.8 5.3 %copy-start.5 = (s32[32]{0:T(128)S(1)}, s32[32]{0:T(128)}, u32[]{:S(2)}) copy-start(s32[32]{0:T(128)} %param.17) | copy-start | bytes 388
  17.8 60.8 %copy-start.1 = (f32[32,256]{1,0:T(8,128)S(1)}, f32[32,256]{1,0:T(8,128)}, u32[]{:S(2)}) copy-start(f32[32,256]{1,0:T(8,128)} %param.14) | copy-start | bytes 98308
  17.8 60.8 %copy-start.2 = (f32[32,256]{1,0:T(8,128)S(1)}, f32[32,256]{1,0:T(8,128)}, u32[]{:S(2)}) copy-start(f32[32,256]{1,0:T(8,128)} %param.15) | copy-start | bytes 98308
  88.0 10.6 %copy-start.3 = (f32[32]{0:T(128)S(1)}, f32[32]{0:T(128)}, u32[]{:S(2)}) copy-start(f32[32]{0:T(128)} %param.19) | copy-start | bytes 388
  93.6 31.9 %copy-start = (f32[32,6,128]{2,0,1:T(8,128)S(1)}, f32[32,6,128]{2,0,1:T(8,128)}, u32[]{:S(2)}) copy-start(f32[32,6,128]{2,0,1:T(8,128)} %param.20) | copy-start | bytes 294916
  99.5 10.4 %all-to-all-start.1 = ((f32[16,3,768]{2,1,0:T(4,128)}), f32[16,3,768]{2,1,0:T(4,128)S(1)}, u32[]{:S(2)}, u32[]{:S(2)}) async-start(f32[16,3,768]{2,1,0:T(4,128)} %copy.160), calls=%async_computation.1 | async-start | bytes 393216 | tf_op jit(solution)/shard_map/all_to_all | solution.py:94
  126.7 10.5 %all-to-all-start.2 = ((f32[16,3,768]{2,1,0:T(4,128)}), f32[16,3,768]{2,1,0:T(4,128)S(1)}, u32[]{:S(2)}, u32[]{:S(2)}) async-start(f32[16,3,768]{2,1,0:T(4,128)} %copy.162), calls=%async_computation.2 | async-start | bytes 393216 | tf_op jit(solution)/shard_map/all_to_all | solution.py:103
  206.6 10.5 %all-to-all-start.4 = ((f32[16,3,768]{2,1,0:T(4,128)}), f32[16,3,768]{2,1,0:T(4,128)S(1)}, u32[]{:S(2)}, u32[]{:S(2)}) async-start(f32[16,3,768]{2,1,0:T(4,128)} %copy.173), calls=%async_computation.4 | async-start | bytes 393216 | tf_op jit(solution)/shard_map/all_to_all | solution.py:103
  286.7 10.5 %all-to-all-start.6 = ((f32[16,3,768]{2,1,0:T(4,128)}), f32[16,3,768]{2,1,0:T(4,128)S(1)}, u32[]{:S(2)}, u32[]{:S(2)}) async-start(f32[16,3,768]{2,1,0:T(4,128)} %copy.184), calls=%async_computation.6 | async-start | bytes 393216 | tf_op jit(solution)/shard_map/all_to_all | solution.py:103
  366.7 10.5 %all-to-all-start.8 = ((f32[16,3,768]{2,1,0:T(4,128)}), f32[16,3,768]{2,1,0:T(4,128)S(1)}, u32[]{:S(2)}, u32[]{:S(2)}) async-start(f32[16,3,768]{2,1,0:T(4,128)} %copy.195), calls=%async_computation.8 | async-start | bytes 393216 | tf_op jit(solution)/shard_map/all_to_all | solution.py:103
  446.4 10.5 %all-to-all-start.10 = ((f32[16,3,768]{2,1,0:T(4,128)}), f32[16,3,768]{2,1,0:T(4,128)S(1)}, u32[]{:S(2)}, u32[]{:S(2)}) async-start(f32[16,3,768]{2,1,0:T(4,128)} %copy.206), calls=%async_computation.10 | async-start | bytes 393216 | tf_op jit(solution)/shard_map/all_to_all | solution.py:103
  476.2 22.0 %copy-start.4 = (f32[2]{0:T(128)S(1)}, f32[2]{0:T(128)}, u32[]{:S(2)}) copy-start(f32[2]{0:T(128)} %constant.79.clone) | copy-start | bytes 28
where the time goes:
time: 503 us; the launch traced here: 499 us
  blocking collectives  189 us (38%)
  other arithmetic  114 us (23%)
  local copies, waits for them, and re-layouts  94 us (19%)
  matrix products  52.6 us (10%)
  starting transfers between devices  30 us (6%)
  waiting for transfers between devices  14.3 us (3%)
  between operations  5.24 us (1%)
    scatter-add x5, other arithmetic, shards(): right_side = (anchor - cost).at[feeder_index, iface_rows].add(penalty * (...  99.9 us
    all_gather x5, blocking collectives, over_pieces(): pieces = lax.all_gather(x, axis)  75.4 us
    psum x8, blocking collectives, over_axes(): return functools.reduce(lax.psum, axes, x)  64.4 us
    all_to_all x4, blocking collectives, shards(): lax.all_to_all(packed, SUB, split_axis=0, concat_axis=0, tiled=True)  48.7 us
    dot_general x5, matrix products, shards(): jnp.einsum('fkj,fjs->fks', inverse, right_side, preferred_element_type=jn...  46 us
    dot_general x5, local copies, waits for them, and re-layouts, shards(): jnp.einsum('fkj,fjs->fks', inverse, right_side, preferred_element_type=jn...  27.9 us
    gather x12, local copies, waits for them, and re-layouts, shards(): boundary = jnp.take_along_axis(primal, iface_rows[:, :, None], axis=1)  23 us
    sub x4, local copies, waits for them, and re-layouts, shards(): anchor - cost  22.3 us
  transfers between devices with their start and end apart: 7, of which 6 were waited for; matrix products, arithmetic and copies ran while one was open for 15% of the time, Pallas kernels for 0%

commit v1 on v0

v1 whole, which is shorter than its diff:
```python
import functools

import jax
import jax.numpy as jnp
from jax import lax
from jax.experimental import pallas as pl
from jax.experimental.pallas import tpu as pltpu
from jax.sharding import Mesh
from jax.sharding import PartitionSpec as P


ITERS = 5
PENALTY = 2.0
AXES = ("sub_0", "sub_1", "fdr_0", "fdr_1")
SUB = ("sub_0", "sub_1")
F, K, C, Q = 32, 256, 128, 6
OWNERS = 3
CHUNK = 4
MESH = pl.DeviceIdType.MESH
f32, bf16, i32 = jnp.float32, jnp.bfloat16, jnp.int32


def ring(d):
    return min(d, 4 - d)


PLANE = sorted(
    ((dx, dz) for dx in range(4) for dz in range(4)),
    key=lambda t: -(ring(t[0]) + ring(t[1])),
)
ALL = sorted(
    (
        (dx, dz, dy, dc)
        for dx in range(4)
        for dz in range(4)
        for dy in range(4)
        for dc in range(2)
    ),
    key=lambda t: -(ring(t[0]) + ring(t[1]) + ring(t[2])),
)[:-2] + [(0, 0, 0, 1)]


def parts(v):
    hi = v.astype(bf16)
    rest = v - hi.astype(f32)
    mid = rest.astype(bf16)
    low = (rest - mid.astype(f32)).astype(bf16)
    return hi, mid, low


def mm(a, b, dims=(((1,), (0,)), ((), ()))):
    return lax.dot_general(a, b, dims, preferred_element_type=f32)


def kernel(
    inv_hbm, cost_hbm, lo_ref, hi_ref, iface, sub, live_ref, weight, target,
    dual_hbm, cons_hbm, norm_ref, set_hbm,
    mat, cost, lob, hib, part0, cols, coef,
    base0, ai, ci, li, hi_i, lcb, sd, out, ri,
    sbuf, cbuf, rep, rbuf, sdo, idbuf, idin, hot, hot_t,
    rwt, den, memb, rows_new, res, resin, consin, cons, dualb, gv, tab, tabs,
    in_sem, tab_sem, id_s, id_r, c_s, c_r, r_s, r_r, n_s, n_r, k_s, k_r, o_sem,
):
    x, z, y, c = [lax.axis_index(a) for a in AXES]
    me = ((x * 4 + z) * 4 + y) * 2 + c
    k_me = x * 4 + z
    own = (c == 1) & (y < OWNERS)
    part = jnp.where(y < OWNERS, y, 0)
    live = live_ref[0]

    def peer(dx, dz, dy, dc):
        t = (lax.rem(x + dx, 4), lax.rem(z + dz, 4), lax.rem(y + dy, 4), lax.rem(c + dc, 2))
        return t, ((t[0] * 4 + t[1]) * 4 + t[2]) * 2 + t[3]

    def wait(view, sem):
        pltpu.make_async_copy(view, view, sem).wait()

    loads = []
    for j in range(F // CHUNK):
        s = pl.ds(j * CHUNK, CHUNK)
        loads.append(
            (
                pltpu.make_async_copy(inv_hbm.at[s], mat.at[s, pl.ds(0, K), :], in_sem.at[0, j]),
                pltpu.make_async_copy(cost_hbm.at[s], cost.at[s], in_sem.at[1, j]),
            )
        )
    for a, b in loads:
        a.start()
        b.start()
    barrier = pltpu.get_barrier_semaphore()
    for d in ALL:
        pl.semaphore_signal(barrier, inc=1, device_id=peer(*d)[0], device_id_type=MESH)

    gv[...] = lax.broadcasted_iota(i32, (C, C), 0) + 1024
    for f in range(F):
        g = jnp.where(f < live, sub[f] // 32, 64 + f)
        gv[f : f + 1, :] = jnp.full((1, C), g, i32)
    grp = gv[...]
    grp_t = grp.T
    row = lax.broadcasted_iota(i32, (C, C), 0)
    lane = lax.broadcasted_iota(i32, (C, C), 1)
    same = grp == grp_t
    rank = jnp.sum(jnp.where(same & (row < lane), 1, 0), axis=0, keepdims=True)
    pos_row = grp_t[0:1] * 3 + rank
    here = jnp.broadcast_to(pos_row, (C, C)).T == lane
    slot_row = jnp.sum(jnp.where(here, row - F, 0), axis=0, keepdims=True) + F
    pos_row = jnp.minimum(pos_row, 47)
    tab[0:1, :] = slot_row
    tab[1:2, :] = pos_row
    to_smem = pltpu.make_async_copy(tab, tabs, tab_sem)
    to_smem.start()

    zero8 = jnp.zeros((F, 8, C), f32)
    for ref in (ci, li, hi_i, lcb, sd):
        ref[...] = zero8
    out[F] = jnp.zeros((8, C), f32)
    to_smem.wait()

    def slot_at(n):
        return jnp.clip(tabs[0, n], 0, F)

    for n in range(48):
        s = slot_at(n)
        number = jnp.where(s < F, (sub[jnp.minimum(s, F - 1)] % 32).astype(f32), -1000.0)
        idbuf[2 * n : 2 * n + 1, :] = jnp.full((1, C), number, f32)
        idbuf[2 * n + 1 : 2 * n + 2, :] = jnp.full((1, C), number + 32.0, f32)

    pl.semaphore_wait(barrier, 127)

    def to_owners(source, dest, first, s_sem, r_sem, self_copy):
        for dx, dz in PLANE:
            tx, tz = lax.rem(x + dx, 4), lax.rem(z + dz, 4)
            k = tx * 4 + tz
            for o in (2, 1, 0):
                copy = pltpu.make_async_remote_copy(
                    source(o, k),
                    dest.at[pl.ds(first + me * 6, 6), :],
                    s_sem,
                    r_sem,
                    device_id=(tx, tz, o, 1),
                    device_id_type=MESH,
                )
                if (dx, dz) == (0, 0):
                    pl.when(jnp.logical_not((y == o) & (c == 1)))(copy.start)
                else:
                    copy.start()

        @pl.when(own)
        def _():
            self_copy()

    def id_self():
        for i in range(6):
            idin[pl.ds(me * 6 + i, 1), :] = idbuf[pl.ds(k_me * 6 + i, 1), :]

    to_owners(lambda o, k: idbuf.at[pl.ds(k * 6, 6), :], idin, 0, id_s, id_r, id_self)

    def wait_48(view, sem):
        @pl.when(own)
        def _():
            wait(view.at[pl.ds(0, 47 * 6), :], sem)

        @pl.when(jnp.logical_not(own))
        def _():
            wait(view.at[pl.ds(0, 48 * 6), :], sem)

    lane16 = lax.broadcasted_iota(i32, (16, K), 1)
    row16 = lax.broadcasted_iota(i32, (16, K), 0)

    def prepare(f):
        at = jnp.full((16, K), -1, i32)
        for q in range(Q):
            at = jnp.where(row16 == q, iface[f, q], at)
        pick32 = jnp.where(lane16 == at, 1.0, 0.0)
        pick = pick32.astype(bf16)
        keep = (1.0 - jnp.sum(pick32, axis=0, keepdims=True)).astype(bf16)
        inverse = mat[f, 0:K, :]
        col = mm(inverse, pick, (((1,), (1,)), ((), ()))).astype(bf16)
        cols[f] = col
        masked = inverse * keep
        mat[f, 0:K, :] = masked
        mat[f, K : K + 16, :] = mm(pick, masked).astype(bf16)
        cross = mm(pick, col)
        for q in range(Q):
            coef[f, q] = jnp.broadcast_to(cross[0:8, q : q + 1], (8, C))
        lob[f] = jnp.broadcast_to(lo_ref[pl.ds(f, 1), :], (C, K)).T
        hib[f] = jnp.broadcast_to(hi_ref[pl.ds(f, 1), :], (C, K)).T
        for q in range(Q):
            r = iface[f, q]
            ci[f, q : q + 1, :] = cost[f, pl.ds(r, 1), :]
            li[f, q : q + 1, :] = lob[f, pl.ds(r, 1), :]
            hi_i[f, q : q + 1, :] = hib[f, pl.ds(r, 1), :]
        ai[f] = -ci[f]
        solve(f, (-cost[f]).astype(bf16))

    def solve(f, base):
        both = mm(mat[f], base)
        part0[f] = both[0:K]
        base0[f] = both[K : K + 8]

    def chunk_loop(body):
        def step(j, carry):
            for i in range(CHUNK):
                body(j * CHUNK + i)
            return carry

        lax.fori_loop(0, F // CHUNK, step, 0)

    for a, b in loads:
        a.wait()
        b.wait()
    chunk_loop(prepare)

    def exchange(t):
        half_at = pl.multiple_of(lax.rem(t, 2) * 768, 768)
        for f in range(F):
            act = jnp.where(f < live, 1.0, 0.0)
            rhs = (ai[f] + PENALTY * (lcb[f] - sd[f])).astype(bf16).astype(f32)
            ri[f] = rhs
            boundary = base0[f]
            for q in range(Q):
                boundary = boundary + coef[f, q] * jnp.broadcast_to(rhs[q : q + 1, :], (8, C))
            out[f] = (boundary + sd[f]) * act
            anchor = jnp.minimum(jnp.maximum(boundary, li[f]), hi_i[f])
            ai[f] = anchor - ci[f]
        for n in range(48):
            v = out[slot_at(n)]
            for o in range(OWNERS):
                sbuf[96 * o + 2 * n : 96 * o + 2 * n + 2, :] = v[2 * o : 2 * o + 2, :]

        def self_copy():
            for i in range(6):
                cbuf[pl.ds(half_at + me * 6 + i, 1), :] = sbuf[pl.ds(part * 96 + k_me * 6 + i, 1), :]

        to_owners(
            lambda o, k: sbuf.at[pl.ds(o * 96 + k * 6, 6), :], cbuf, half_at, c_s, c_r, self_copy
        )

        def primal_of(f):
            primal = part0[f] + mm(cols[f, :, 0:8], ri[f].astype(bf16))
            return jnp.minimum(jnp.maximum(primal, lob[f]), hib[f])

        @pl.when(t < ITERS - 1)
        def _():
            def advance(f):
                solve(f, (primal_of(f) - cost[f]).astype(bf16))

            chunk_loop(advance)

        @pl.when(t == ITERS - 1)
        def _():
            def last(f):
                part0[f] = primal_of(f) * jnp.where(f < live, 1.0, 0.0)

            chunk_loop(last)
            pltpu.make_async_copy(part0, set_hbm, o_sem.at[0]).start()

        @pl.when(own & (t == 0))
        def _():
            wait(idin.at[pl.ds(0, 127 * 6), :], id_r)
            lanes = lax.broadcasted_iota(i32, (768, 256), 1)
            want = jnp.where(lanes < 192, lax.rem(lanes, 64), -1).astype(f32)
            ids = idin[...]
            h = jnp.where(jnp.concatenate([ids, ids], axis=1) == want, 1.0, 0.0)
            hot[...] = h.astype(bf16)
            ht = h[:, 0:C].T[0:64, :]
            hot_t[...] = ht.astype(bf16)
            count = mm(ht.astype(bf16), jnp.ones((768, C), bf16))
            memb[...] = count
            for s in range(32):
                w = weight[s]
                for q in range(2):
                    r = s + 32 * q
                    rwt[r : r + 1, :] = w * target[s, pl.ds(2 * part + q, 1), :]
                    den[r : r + 1, :] = memb[r : r + 1, :] + w
            sdo[...] = jnp.zeros((768, C), f32)
            rows_new[...] = jnp.zeros((64, C), f32)
            res[...] = jnp.zeros((8, C), f32)

        @pl.when(own)
        def _():
            wait(cbuf.at[pl.ds(half_at, 127 * 6), :], c_r)
            arrived = cbuf.at[pl.ds(half_at, 768), :]
            sums = None
            for a in parts(arrived[...]):
                term = mm(hot_t[...], a)
                sums = term if sums is None else sums + term
            new = (sums + rwt[...]) / den[...]
            diff = new - rows_new[...]
            rows_new[...] = new
            triple = jnp.concatenate([*parts(new), jnp.zeros((64, C), bf16)], axis=0)
            back = mm(hot[...], triple)
            rep[...] = back
            for d in ALL:
                to, number = peer(*d)
                pltpu.make_async_remote_copy(
                    rep.at[pl.ds(number * 6, 6), :],
                    rbuf.at[pl.ds(part * 96 + k_me * 6, 6), :],
                    r_s,
                    r_r,
                    device_id=to,
                    device_id_type=MESH,
                ).start()
            for i in range(6):
                rbuf[pl.ds(part * 96 + k_me * 6 + i, 1), :] = rep[pl.ds(me * 6 + i, 1), :]
            next_sd = arrived[...] - rep[...]
            miss = next_sd - sdo[...]
            sdo[...] = next_sd
            primal_sum = jnp.sum(miss * miss, axis=0, keepdims=True)
            dual_sum = jnp.sum(memb[...] * (diff * diff), axis=0, keepdims=True)
            half = lax.broadcasted_iota(i32, (1, C), 1) < 64
            folded = jnp.where(
                half,
                primal_sum + pltpu.roll(primal_sum, 64, 1),
                dual_sum + pltpu.roll(dual_sum, 64, 1),
            )
            res[...] = jnp.where(lax.broadcasted_iota(i32, (8, C), 0) == t, folded, res[...])

            @pl.when(t == ITERS - 1)
            def _():
                for dx, dz, dy, dc in ALL:
                    to, number = peer(dx, dz, dy, dc)
                    if (dx, dz) == (0, 0):
                        pltpu.make_async_remote_copy(
                            rows_new, consin.at[part], k_s, k_r, device_id=to, device_id_type=MESH
                        ).start()
                    pltpu.make_async_remote_copy(
                        res, resin.at[part * 16 + k_me], n_s, n_r, device_id=to, device_id_type=MESH
                    ).start()
                resin[part * 16 + k_me] = res[...]
                consin[part] = rows_new[...]

            wait(rep.at[pl.ds(0, 127 * 6), :], r_s)

        wait_48(rbuf, r_r)

        for f in range(F):
            at = 2 * jnp.clip(tabs[1, f], 0, 47)
            for o in range(OWNERS):
                for q in range(2):
                    r = 2 * o + q
                    lcb[f, r : r + 1, :] = rbuf[pl.ds(96 * o + at + q, 1), :]
        for f in range(F):
            act = jnp.where(f < live, 1.0, 0.0)
            sd[f] = out[f] - lcb[f] * act

        wait_48(sbuf, c_s)
        return 0

    lax.fori_loop(0, ITERS, lambda t, carry: exchange(t), 0)

    dualb[...] = PENALTY * sd[:, 0:Q, :]
    dual_out = pltpu.make_async_copy(dualb, dual_hbm, o_sem.at[1])
    dual_out.start()

    @pl.when(own)
    def _():
        wait(consin.at[pl.ds(0, 2)], k_r)
        wait(resin.at[pl.ds(0, 47)], n_r)

    @pl.when(jnp.logical_not(own))
    def _():
        wait(consin, k_r)
        wait(resin, n_r)

    for o in range(OWNERS):
        for q in range(2):
            cons[:, 2 * o + q, :] = consin[o, 32 * q : 32 * q + 32, :]
    cons_out = pltpu.make_async_copy(cons, cons_hbm, o_sem.at[2])
    cons_out.start()
    total = jnp.sum(resin[...], axis=0)
    lane8 = lax.broadcasted_iota(i32, (8, C), 1)
    primal = jnp.sum(jnp.where(lane8 < 64, total, 0.0), axis=1, keepdims=True)
    dual = jnp.sum(jnp.where(lane8 < 64, 0.0, total), axis=1, keepdims=True)
    norms = jnp.where(lane8 == 0, jnp.sqrt(primal), PENALTY * jnp.sqrt(dual))
    norm_ref[...] = norms[0:ITERS, 0:2]

    @pl.when(own)
    def _():
        wait(cbuf.at[pl.ds(0, 7 * 64), :], k_s)
        wait(cbuf.at[pl.ds(0, 127 * 8), :], n_s)

    wait_48(idin, id_s)
    pltpu.make_async_copy(part0, set_hbm, o_sem.at[0]).wait()
    dual_out.wait()
    cons_out.wait()


def shards(*operands):
    vmem = functools.partial(pltpu.VMEM, dtype=f32)
    anyspace = pl.BlockSpec(memory_space=pl.ANY)
    on_vmem = pl.BlockSpec(memory_space=pltpu.VMEM)
    on_smem = pl.BlockSpec(memory_space=pltpu.SMEM)
    dma = pltpu.SemaphoreType.DMA
    return pl.pallas_call(
        kernel,
        out_shape=(
            jax.ShapeDtypeStruct((F, Q, C), f32),
            jax.ShapeDtypeStruct((32, Q, C), f32),
            jax.ShapeDtypeStruct((ITERS, 2), f32),
            jax.ShapeDtypeStruct((F, K, C), f32),
        ),
        in_specs=[anyspace, anyspace, on_vmem, on_vmem, on_smem, on_smem, on_smem, on_smem, on_vmem],
        out_specs=(anyspace, anyspace, on_vmem, anyspace),
        scratch_shapes=[
            pltpu.VMEM((F, K + 16, K), bf16),
            vmem((F, K, C)),
            vmem((F, K, C)),
            vmem((F, K, C)),
            vmem((F, K, C)),
            pltpu.VMEM((F, K, 16), bf16),
            vmem((F, Q, 8, C)),
            vmem((F, 8, C)),
            vmem((F, 8, C)),
            vmem((F, 8, C)),
            vmem((F, 8, C)),
            vmem((F, 8, C)),
            vmem((F, 8, C)),
            vmem((F, 8, C)),
            vmem((F + 1, 8, C)),
            vmem((F, 8, C)),
            vmem((OWNERS * 96, C)),
            vmem((2 * 768, C)),
            vmem((768, C)),
            vmem((OWNERS * 96, C)),
            vmem((768, C)),
            vmem((96, C)),
            vmem((768, C)),
            pltpu.VMEM((768, 256), bf16),
            pltpu.VMEM((64, 768), bf16),
            vmem((64, C)),
            vmem((64, C)),
            vmem((64, C)),
            vmem((64, C)),
            vmem((8, C)),
            vmem((48, 8, C)),
            vmem((OWNERS, 64, C)),
            vmem((32, Q, C)),
            vmem((F, Q, C)),
            pltpu.VMEM((C, C), i32),
            pltpu.VMEM((2, C), i32),
            pltpu.SMEM((2, C), i32),
            dma((2, F // CHUNK)),
            dma,
            dma,
            dma,
            dma,
            dma,
            dma,
            dma,
            dma,
            dma,
            dma,
            dma,
            dma((3,)),
        ],
        compiler_params=pltpu.CompilerParams(
            collective_id=0, has_side_effects=True, vmem_limit_bytes=58 * 2**20
        ),
    )(*operands)


def solution(mesh):
    torus = Mesh(mesh.devices.reshape(4, 4, 4, 2), AXES)
    placed = (
        P(AXES, None, None),
        P(AXES, None, None),
        P(AXES, None),
        P(AXES, None),
        P(AXES, None),
        P(AXES),
        P(AXES),
        P(SUB),
        P(SUB, None, None),
    )
    return jax.shard_map(
        shards,
        mesh=torus,
        in_specs=placed,
        out_specs=(P(AXES, None, None), P(SUB, None, None), P(), P(AXES, None, None)),
        check_vma=False,
    )
```

time: 503 us -> 99.8 us (0.20)
  blocking collectives: 189 us -> 0 us
  other arithmetic: 114 us -> 0 us
  Pallas kernels: 0 us -> 86.1 us
  local copies, waits for them, and re-layouts: 94 us -> 12.1 us
  matrix products: 52.6 us -> 0 us
  starting transfers between devices: 30 us -> 0 us
  waiting for transfers between devices: 14.3 us -> 0 us
    scatter-add x5 -> x0, other arithmetic: 99.9 us -> none  [shards(): right_side = (anchor - cost).at[feeder_index, iface_rows].add(penalty * (...]
    pallas_call x0 -> x1, Pallas kernels: none -> 86.1 us  [shards(): pl.pallas_call(kernel, out_shape=(jax.ShapeDtypeStruct((F, Q, C), f32), j...]
    all_gather x5 -> x0, blocking collectives: 75.4 us -> none  [over_pieces(): pieces = lax.all_gather(x, axis)]
    psum x8 -> x0, blocking collectives: 64.4 us -> none  [over_axes(): return functools.reduce(lax.psum, axes, x)]
    dot_general x25 -> x0, matrix products: 52.6 us -> none  [the longest x5 46 us: shards(): jnp.einsum('fkj,fjs->fks', inverse, right_side, preferred_element_type=jn...]
    all_to_all x4 -> x0, blocking collectives: 48.7 us -> none  [shards(): lax.all_to_all(packed, SUB, split_axis=0, concat_axis=0, tiled=True)]
    dot_general x15 -> x0, local copies, waits for them, and re-layouts: 33 us -> none  [the longest x5 27.9 us: shards(): jnp.einsum('fkj,fjs->fks', inverse, right_side, preferred_element_type=jn...]
    all_to_all x7 -> x0, starting transfers between devices: 30 us -> none  [the longest x5 18 us: shards(): lax.all_to_all(reply, SUB, split_axis=0, concat_axis=0, tiled=True)]
  transfers between devices with their start and end apart: 7 -> 0, of which waited for: 6 -> 0; matrix products, arithmetic and copies ran while one was open for 15% -> 0% of each run, Pallas kernels for 0% -> 0%
where the time goes in v1:
time: 99.8 us; the launch traced here: 99.5 us
  Pallas kernels  86.1 us (86%)
  local copies, waits for them, and re-layouts  12.1 us (12%)
  between operations  1.29 us (1%)
    pallas_call x1, Pallas kernels, shards(): pl.pallas_call(kernel, out_shape=(jax.ShapeDtypeStruct((F, Q, C), f32), j...  86.1 us
    unnamed x3, local copies, waits for them, and re-layouts  7.63 us
    pallas_call x3, local copies, waits for them, and re-layouts, shards(): pl.pallas_call(kernel, out_shape=(jax.ShapeDtypeStruct((F, Q, C), f32), j...  4.45 us

profile of v1, /device:TPU:1, one launch (start us, length us, event | category | flops | bytes accessed | tf_op | source)
XLA Modules:
  0.0 99.5 jit_solution(1869704421306333042)
XLA Ops:
  1.3 1.4 %copy.13.iface = s32[32,6]{1,0:T(8,128)} copy(s32[32,6]{0,1:T(8,128)} %param.13) | data formatting | bytes 1536 | tf_op args[4]
  2.7 1.6 %copy.14.target = f32[32,6,128]{2,1,0:T(8,128)} copy(f32[32,6,128]{2,0,1:T(8,128)} %param.17) | data formatting | bytes 196608 | tf_op args[8]
  4.3 86.1 %shard_map.120 = (f32[32,6,128]{2,1,0:T(8,128)}, f32[32,6,128]{2,1,0:T(8,128)}, f32[5,2]{1,0:T(8,128)}, f32[32,256,128]{2,1,0:T(8,128)}) custom-call(bf16[32,256,256]{2,1,0:T(8,128)(2,1)} %inv_hbm.1, f32[32,256,128]{2,1,0:T(8,128)} %cost_hbm.1, f32[32,256]{1,0:T(8,128)} %lo_ref.1, f32[32,256]{1,0:T(8,128)} %hi_ref.1, s32[32,6]{1,0:T(8,128)} %copy.13.iface, ...), custom_call_target="tpu_custom_call" | custom-call | tf_op jit(solution)/shard_map/pallas_call | solution.py:395
  90.4 1.6 %copy.15 = f32[32,6,128]{2,0,1:T(8,128)} copy(f32[32,6,128]{2,1,0:T(8,128)} %get-tuple-element.4) | data formatting | bytes 196608 | tf_op jit(solution)/shard_map/pallas_call | solution.py:395
  92.0 1.3 %copy.17 = f32[5,2]{0,1:T(2,128)} copy(f32[5,2]{1,0:T(8,128)} %get-tuple-element.6) | data formatting | bytes 80 | tf_op jit(solution)/shard_map/pallas_call | solution.py:395
  93.3 1.6 %copy.16 = f32[32,6,128]{2,0,1:T(8,128)} copy(f32[32,6,128]{2,1,0:T(8,128)} %get-tuple-element.5) | data formatting | bytes 196608 | tf_op jit(solution)/shard_map/pallas_call | solution.py:395
  94.9 4.7 %copy.20 = f32[32,256,128]{2,1,0:T(8,128)} copy(f32[32,256,128]{2,1,0:T(8,128)} %get-tuple-element.15) | data formatting | bytes 8388608

commit v2 on v1

--- a/solution.py
+++ b/solution.py
@@ -15,8 +15,9 @@
 SUB = ("sub_0", "sub_1")
 F, K, C, Q = 32, 256, 128, 6
 OWNERS = 3
-CHUNK = 4
+CHUNK = 8
 MESH = pl.DeviceIdType.MESH
+NT = (((1,), (1,)), ((), ()))
 f32, bf16, i32 = jnp.float32, jnp.bfloat16, jnp.int32
 
 
@@ -53,20 +54,20 @@
 
 
 def kernel(
-    inv_hbm, cost_hbm, lo_ref, hi_ref, iface, sub, live_ref, weight, target,
-    dual_hbm, cons_hbm, norm_ref, set_hbm,
-    mat, cost, lob, hib, part0, cols, coef,
+    inv_hbm, cost_hbm, lo_hbm, hi_hbm, iface_hbm, sub_hbm, live_hbm, weight_hbm, target_hbm,
+    dual_ref, cons_ref, norm_ref, part0,
+    mat, cost, lob, hib, cols, coef,
     base0, ai, ci, li, hi_i, lcb, sd, out, ri,
     sbuf, cbuf, rep, rbuf, sdo, idbuf, idin, hot, hot_t,
-    rwt, den, memb, rows_new, res, resin, consin, cons, dualb, gv, tab, tabs,
-    in_sem, tab_sem, id_s, id_r, c_s, c_r, r_s, r_r, n_s, n_r, k_s, k_r, o_sem,
+    rwt, den, memb, rows_new, res, resin, consin, gv, tab, tabs,
+    lo_ref, hi_ref, iface, sub, live_ref, weight, target, bnd,
+    in_sem, arg_sem, tab_sem, id_s, id_r, c_s, c_r, r_s, r_r, n_s, n_r, k_s, k_r,
 ):
     x, z, y, c = [lax.axis_index(a) for a in AXES]
     me = ((x * 4 + z) * 4 + y) * 2 + c
     k_me = x * 4 + z
     own = (c == 1) & (y < OWNERS)
     part = jnp.where(y < OWNERS, y, 0)
-    live = live_ref[0]
 
     def peer(dx, dz, dy, dc):
         t = (lax.rem(x + dx, 4), lax.rem(z + dz, 4), lax.rem(y + dy, 4), lax.rem(c + dc, 2))
@@ -75,21 +76,42 @@
     def wait(view, sem):
         pltpu.make_async_copy(view, view, sem).wait()
 
-    loads = []
-    for j in range(F // CHUNK):
-        s = pl.ds(j * CHUNK, CHUNK)
-        loads.append(
+    small = [
+        pltpu.make_async_copy(a, b, arg_sem.at[i])
+        for i, (a, b) in enumerate(
             (
-                pltpu.make_async_copy(inv_hbm.at[s], mat.at[s, pl.ds(0, K), :], in_sem.at[0, j]),
-                pltpu.make_async_copy(cost_hbm.at[s], cost.at[s], in_sem.at[1, j]),
+                (sub_hbm, sub),
+                (live_hbm, live_ref),
+                (iface_hbm, iface),
+                (weight_hbm, weight),
+                (lo_hbm, lo_ref),
+                (hi_hbm, hi_ref),
+                (target_hbm, target),
             )
         )
-    for a, b in loads:
-        a.start()
-        b.start()
+    ]
+
+    def loads(j):
+        s = pl.ds(j * CHUNK, CHUNK)
+        return (
+            pltpu.make_async_copy(inv_hbm.at[s], mat.at[s, pl.ds(0, K), :], in_sem.at[0, j]),
+            pltpu.make_async_copy(cost_hbm.at[s], cost.at[s], in_sem.at[1, j]),
+        )
+
+    for copy in small[:3]:
+        copy.start()
+    for j in range(F // CHUNK):
+        for copy in loads(j):
+            copy.start()
+    for copy in small[3:]:
+        copy.start()
     barrier = pltpu.get_barrier_semaphore()
     for d in ALL:
         pl.semaphore_signal(barrier, inc=1, device_id=peer(*d)[0], device_id_type=MESH)
+
+    for copy in small[:3]:
+        copy.wait()
+    live = live_ref[0]
 
     gv[...] = lax.broadcasted_iota(i32, (C, C), 0) + 1024
     for f in range(F):
@@ -111,21 +133,12 @@
     to_smem.start()
 
     zero8 = jnp.zeros((F, 8, C), f32)
-    for ref in (ci, li, hi_i, lcb, sd):
+    for ref in (ai, ci, li, hi_i, lcb, sd):
         ref[...] = zero8
+    coef[...] = jnp.zeros((F, Q, 8, C), f32)
     out[F] = jnp.zeros((8, C), f32)
-    to_smem.wait()
-
     def slot_at(n):
         return jnp.clip(tabs[0, n], 0, F)
-
-    for n in range(48):
-        s = slot_at(n)
-        number = jnp.where(s < F, (sub[jnp.minimum(s, F - 1)] % 32).astype(f32), -1000.0)
-        idbuf[2 * n : 2 * n + 1, :] = jnp.full((1, C), number, f32)
-        idbuf[2 * n + 1 : 2 * n + 2, :] = jnp.full((1, C), number + 32.0, f32)
-
-    pl.semaphore_wait(barrier, 127)
 
     def to_owners(source, dest, first, s_sem, r_sem, self_copy):
         for dx, dz in PLANE:
@@ -149,12 +162,6 @@
         def _():
             self_copy()
 
-    def id_self():
-        for i in range(6):
-            idin[pl.ds(me * 6 + i, 1), :] = idbuf[pl.ds(k_me * 6 + i, 1), :]
-
-    to_owners(lambda o, k: idbuf.at[pl.ds(k * 6, 6), :], idin, 0, id_s, id_r, id_self)
-
     def wait_48(view, sem):
         @pl.when(own)
         def _():
@@ -167,49 +174,76 @@
     lane16 = lax.broadcasted_iota(i32, (16, K), 1)
     row16 = lax.broadcasted_iota(i32, (16, K), 0)
 
-    def prepare(f):
+    def picks(f):
         at = jnp.full((16, K), -1, i32)
         for q in range(Q):
-            at = jnp.where(row16 == q, iface[f, q], at)
-        pick32 = jnp.where(lane16 == at, 1.0, 0.0)
-        pick = pick32.astype(bf16)
-        keep = (1.0 - jnp.sum(pick32, axis=0, keepdims=True)).astype(bf16)
-        inverse = mat[f, 0:K, :]
-        col = mm(inverse, pick, (((1,), (1,)), ((), ()))).astype(bf16)
-        cols[f] = col
-        masked = inverse * keep
-        mat[f, 0:K, :] = masked
-        mat[f, K : K + 16, :] = mm(pick, masked).astype(bf16)
-        cross = mm(pick, col)
+            at = jnp.where(row16 == q, iface[q, f], at)
+        pick = jnp.where(lane16 == at, 1.0, 0.0)
+        return pick.astype(bf16), 1.0 - jnp.sum(pick, axis=0, keepdims=True)
+
+    def prepare(f):
+        pick, _ = picks(f)
+        rows = mm(pick, mat[f, 0:K, :]).astype(bf16)
+        mat[f, K : K + 16, :] = rows
+        base0[f] = mm(rows, (-cost[f]).astype(bf16))[0:8]
+
+    def complete(f):
+        pick, keep = picks(f)
+        cols[f] = mm(mat[f, 0:K, :], pick, NT).astype(bf16)
+        rows = mat[f, K : K + 16, :]
+        cross = mm(rows, pick, NT)
+        mat[f, K : K + 16, :] = rows * keep.astype(bf16)
         for q in range(Q):
             coef[f, q] = jnp.broadcast_to(cross[0:8, q : q + 1], (8, C))
         lob[f] = jnp.broadcast_to(lo_ref[pl.ds(f, 1), :], (C, K)).T
         hib[f] = jnp.broadcast_to(hi_ref[pl.ds(f, 1), :], (C, K)).T
         for q in range(Q):
-            r = iface[f, q]
+            r = iface[q, f]
             ci[f, q : q + 1, :] = cost[f, pl.ds(r, 1), :]
             li[f, q : q + 1, :] = lob[f, pl.ds(r, 1), :]
             hi_i[f, q : q + 1, :] = hib[f, pl.ds(r, 1), :]
-        ai[f] = -ci[f]
-        solve(f, (-cost[f]).astype(bf16))
+
+    def first(f):
+        _, keep = picks(f)
+        inverse = mat[f, 0:K, :]
+        primal = mm(inverse, (-cost[f]).astype(bf16))
+        mat[f, 0:K, :] = inverse * keep.astype(bf16)
+        anchor = jnp.minimum(jnp.maximum(primal, lob[f]), hib[f])
+        solve(f, (anchor - cost[f]).astype(bf16))
 
     def solve(f, base):
         both = mm(mat[f], base)
         part0[f] = both[0:K]
         base0[f] = both[K : K + 8]
 
-    def chunk_loop(body):
+    def chunk_loop(body, arrive=False):
         def step(j, carry):
+            if arrive:
+                for copy in loads(j):
+                    copy.wait()
             for i in range(CHUNK):
                 body(j * CHUNK + i)
             return carry
 
         lax.fori_loop(0, F // CHUNK, step, 0)
 
-    for a, b in loads:
-        a.wait()
-        b.wait()
-    chunk_loop(prepare)
+    chunk_loop(prepare, arrive=True)
+
+    to_smem.wait()
+    for n in range(48):
+        s = slot_at(n)
+        number = jnp.where(s < F, (sub[jnp.minimum(s, F - 1)] % 32).astype(f32), -1000.0)
+        idbuf[2 * n : 2 * n + 1, :] = jnp.full((1, C), number, f32)
+        idbuf[2 * n + 1 : 2 * n + 2, :] = jnp.full((1, C), number + 32.0, f32)
+    pl.semaphore_wait(barrier, 127)
+
+    def id_self():
+        for i in range(6):
+            idin[pl.ds(me * 6 + i, 1), :] = idbuf[pl.ds(k_me * 6 + i, 1), :]
+
+    to_owners(lambda o, k: idbuf.at[pl.ds(k * 6, 6), :], idin, 0, id_s, id_r, id_self)
+    for copy in small[3:]:
+        copy.wait()
 
     def exchange(t):
         half_at = pl.multiple_of(lax.rem(t, 2) * 768, 768)
@@ -221,8 +255,7 @@
             for q in range(Q):
                 boundary = boundary + coef[f, q] * jnp.broadcast_to(rhs[q : q + 1, :], (8, C))
             out[f] = (boundary + sd[f]) * act
-            anchor = jnp.minimum(jnp.maximum(boundary, li[f]), hi_i[f])
-            ai[f] = anchor - ci[f]
+            bnd[f] = boundary
         for n in range(48):
             v = out[slot_at(n)]
             for o in range(OWNERS):
@@ -240,7 +273,11 @@
             primal = part0[f] + mm(cols[f, :, 0:8], ri[f].astype(bf16))
             return jnp.minimum(jnp.maximum(primal, lob[f]), hib[f])
 
-        @pl.when(t < ITERS - 1)
+        @pl.when(t == 0)
+        def _():
+            chunk_loop(complete)
+
+        @pl.when((t > 0) & (t < ITERS - 1))
         def _():
             def advance(f):
                 solve(f, (primal_of(f) - cost[f]).astype(bf16))
@@ -253,7 +290,6 @@
                 part0[f] = primal_of(f) * jnp.where(f < live, 1.0, 0.0)
 
             chunk_loop(last)
-            pltpu.make_async_copy(part0, set_hbm, o_sem.at[0]).start()
 
         @pl.when(own & (t == 0))
         def _():
@@ -271,11 +307,14 @@
                 w = weight[s]
                 for q in range(2):
                     r = s + 32 * q
-                    rwt[r : r + 1, :] = w * target[s, pl.ds(2 * part + q, 1), :]
+                    rwt[r : r + 1, :] = w * target[2 * part + q, s : s + 1, :]
                     den[r : r + 1, :] = memb[r : r + 1, :] + w
             sdo[...] = jnp.zeros((768, C), f32)
             rows_new[...] = jnp.zeros((64, C), f32)
-            res[...] = jnp.zeros((8, C), f32)
+            res[...] = jnp.zeros((1, C), f32)
+
+        for f in range(F):
+            ai[f] = jnp.minimum(jnp.maximum(bnd[f], li[f]), hi_i[f]) - ci[f]
 
         @pl.when(own)
         def _():
@@ -308,13 +347,10 @@
             sdo[...] = next_sd
             primal_sum = jnp.sum(miss * miss, axis=0, keepdims=True)
             dual_sum = jnp.sum(memb[...] * (diff * diff), axis=0, keepdims=True)
-            half = lax.broadcasted_iota(i32, (1, C), 1) < 64
-            folded = jnp.where(
-                half,
-                primal_sum + pltpu.roll(primal_sum, 64, 1),
-                dual_sum + pltpu.roll(dual_sum, 64, 1),
-            )
-            res[...] = jnp.where(lax.broadcasted_iota(i32, (8, C), 0) == t, folded, res[...])
+            lane1 = lax.broadcasted_iota(i32, (1, C), 1)
+            for at, value in ((t, primal_sum), (t + 64, dual_sum)):
+                value = jnp.broadcast_to(jnp.sum(value, axis=1, keepdims=True), (1, C))
+                res[...] = jnp.where(lane1 == at, value, res[...])
 
             @pl.when(t == ITERS - 1)
             def _():
@@ -325,12 +361,16 @@
                             rows_new, consin.at[part], k_s, k_r, device_id=to, device_id_type=MESH
                         ).start()
                     pltpu.make_async_remote_copy(
-                        res, resin.at[part * 16 + k_me], n_s, n_r, device_id=to, device_id_type=MESH
+                        res, resin.at[pl.ds(part * 16 + k_me, 1), :], n_s, n_r, device_id=to, device_id_type=MESH
                     ).start()
-                resin[part * 16 + k_me] = res[...]
+                resin[pl.ds(part * 16 + k_me, 1), :] = res[...]
                 consin[part] = rows_new[...]
 
             wait(rep.at[pl.ds(0, 127 * 6), :], r_s)
+
+        @pl.when(t == 0)
+        def _():
+            chunk_loop(first)
 
         wait_48(rbuf, r_r)
 
@@ -349,14 +389,13 @@
 
     lax.fori_loop(0, ITERS, lambda t, carry: exchange(t), 0)
 
-    dualb[...] = PENALTY * sd[:, 0:Q, :]
-    dual_out = pltpu.make_async_copy(dualb, dual_hbm, o_sem.at[1])
-    dual_out.start()
+    for q in range(Q):
+        dual_ref[q] = PENALTY * sd[:, q, :]
 
     @pl.when(own)
     def _():
         wait(consin.at[pl.ds(0, 2)], k_r)
-        wait(resin.at[pl.ds(0, 47)], n_r)
+        wait(resin.at[pl.ds(0, 47), :], n_r)
 
     @pl.when(jnp.logical_not(own))
     def _():
@@ -365,46 +404,33 @@
 
     for o in range(OWNERS):
         for q in range(2):
-            cons[:, 2 * o + q, :] = consin[o, 32 * q : 32 * q + 32, :]
-    cons_out = pltpu.make_async_copy(cons, cons_hbm, o_sem.at[2])
-    cons_out.start()
-    total = jnp.sum(resin[...], axis=0)
-    lane8 = lax.broadcasted_iota(i32, (8, C), 1)
-    primal = jnp.sum(jnp.where(lane8 < 64, total, 0.0), axis=1, keepdims=True)
-    dual = jnp.sum(jnp.where(lane8 < 64, 0.0, total), axis=1, keepdims=True)
-    norms = jnp.where(lane8 == 0, jnp.sqrt(primal), PENALTY * jnp.sqrt(dual))
-    norm_ref[...] = norms[0:ITERS, 0:2]
+            cons_ref[2 * o + q] = consin[o, 32 * q : 32 * q + 32, :]
+    root = jnp.sqrt(jnp.sum(resin[...], axis=0, keepdims=True))
+    norm_ref[0:1, :] = root[:, 0:ITERS]
+    norm_ref[1:2, :] = PENALTY * root[:, 64 : 64 + ITERS]
 
     @pl.when(own)
     def _():
         wait(cbuf.at[pl.ds(0, 7 * 64), :], k_s)
-        wait(cbuf.at[pl.ds(0, 127 * 8), :], n_s)
+        wait(cbuf.at[pl.ds(0, 127), :], n_s)
 
     wait_48(idin, id_s)
-    pltpu.make_async_copy(part0, set_hbm, o_sem.at[0]).wait()
-    dual_out.wait()
-    cons_out.wait()
-
-
-def shards(*operands):
+
+
+def shards(inverse, cost, lower, upper, iface, sub, live, weight, target):
+    operands = (inverse, cost, lower, upper, iface.T, sub, live, weight, target.transpose(1, 0, 2))
     vmem = functools.partial(pltpu.VMEM, dtype=f32)
     anyspace = pl.BlockSpec(memory_space=pl.ANY)
     on_vmem = pl.BlockSpec(memory_space=pltpu.VMEM)
-    on_smem = pl.BlockSpec(memory_space=pltpu.SMEM)
     dma = pltpu.SemaphoreType.DMA
-    return pl.pallas_call(
+    shapes = ((Q, F, C), (Q, 32, C), (2, ITERS), (F, K, C))
+    duals, consensus, norms, setpoints = pl.pallas_call(
         kernel,
-        out_shape=(
-            jax.ShapeDtypeStruct((F, Q, C), f32),
-            jax.ShapeDtypeStruct((32, Q, C), f32),
-            jax.ShapeDtypeStruct((ITERS, 2), f32),
-            jax.ShapeDtypeStruct((F, K, C), f32),
-        ),
-        in_specs=[anyspace, anyspace, on_vmem, on_vmem, on_smem, on_smem, on_smem, on_smem, on_vmem],
-        out_specs=(anyspace, anyspace, on_vmem, anyspace),
+        out_shape=tuple(vmem(shape) for shape in shapes),
+        in_specs=[anyspace] * 9,
+        out_specs=(on_vmem,) * 4,
         scratch_shapes=[
             pltpu.VMEM((F, K + 16, K), bf16),
-            vmem((F, K, C)),
             vmem((F, K, C)),
             vmem((F, K, C)),
             vmem((F, K, C)),
@@ -432,32 +458,39 @@
             vmem((64, C)),
             vmem((64, C)),
             vmem((64, C)),
-            vmem((8, C)),
-            vmem((48, 8, C)),
+            vmem((1, C)),
+            vmem((48, C)),
             vmem((OWNERS, 64, C)),
-            vmem((32, Q, C)),
-            vmem((F, Q, C)),
             pltpu.VMEM((C, C), i32),
             pltpu.VMEM((2, C), i32),
             pltpu.SMEM((2, C), i32),
+            vmem((F, K)),
+            vmem((F, K)),
+            pltpu.SMEM((Q, F), i32),
+            pltpu.SMEM((F,), i32),
+            pltpu.SMEM((1,), i32),
+            pltpu.SMEM((32,), f32),
+            vmem((Q, 32, C)),
+            vmem((F, 8, C)),
             dma((2, F // CHUNK)),
-            dma,
-            dma,
-            dma,
-            dma,
-            dma,
-            dma,
-            dma,
-            dma,
-            dma,
-            dma,
-            dma,
-            dma((3,)),
+            dma((7,)),
+            dma,
+            dma,
+            dma,
+            dma,
+            dma,
+            dma,
+            dma,
+            dma,
+            dma,
+            dma,
+            dma,
         ],
         compiler_params=pltpu.CompilerParams(
             collective_id=0, has_side_effects=True, vmem_limit_bytes=58 * 2**20
         ),
     )(*operands)
+    return duals.transpose(1, 0, 2), consensus.transpose(1, 0, 2), norms.T, setpoints
 
 
 def solution(mesh):

time: 99.8 us -> 83.4 us (0.84)
  local copies, waits for them, and re-layouts: 12.1 us -> 3.86 us
  Pallas kernels: 86.1 us -> 78.2 us
    pallas_call x1, Pallas kernels: 86.1 us -> 78.2 us  [shards(): pl.pallas_call(kernel, out_shape=tuple((vmem(shape) for shape in shapes))...]
    pallas_call x3 -> x0, local copies, waits for them, and re-layouts: 4.45 us -> none  [shards(): pl.pallas_call(kernel, out_shape=(jax.ShapeDtypeStruct((F, Q, C), f32), j...]
    unnamed x3 -> x4, local copies, waits for them, and re-layouts: 7.63 us -> 3.86 us
where the time goes in v2:
time: 83.4 us; the launch traced here: 83.3 us
  Pallas kernels  78.2 us (94%)
  local copies, waits for them, and re-layouts  3.86 us (5%)
  between operations  1.29 us (2%)
    pallas_call x1, Pallas kernels, shards(): pl.pallas_call(kernel, out_shape=tuple((vmem(shape) for shape in shapes))...  78.2 us
    unnamed x4, local copies, waits for them, and re-layouts  3.86 us

profile of v2, /device:TPU:1, one launch (start us, length us, event | category | flops | bytes accessed | tf_op | source)
XLA Modules:
  0.0 83.3 jit_solution(9633555380099256691)
XLA Ops:
  1.3 78.2 %shard_map.120 = (f32[6,32,128]{2,1,0:T(8,128)S(1)}, f32[6,32,128]{2,1,0:T(8,128)S(1)}, f32[2,5]{1,0:T(2,128)S(1)}, f32[32,256,128]{2,1,0:T(8,128)S(1)}) custom-call(bf16[32,256,256]{2,1,0:T(8,128)(2,1)} %inv_hbm.1, f32[32,256,128]{2,1,0:T(8,128)} %cost_hbm.1, f32[32,256]{1,0:T(8,128)} %lo_hbm.1, f32[32,256]{1,0:T(8,128)} %hi_hbm.1, s32[6,32]{1,0:T(8,128)} %bitcast.9, ...), custom_call_target="tpu_custom_call" | custom-call | tf_op jit(solution)/shard_map/pallas_call | solution.py:427
  79.5 0.6 copy.17
  80.1 0.6 copy.18
  80.8 0.6 copy.19
  81.3 2.0 %copy.20 = f32[32,256,128]{2,1,0:T(8,128)} copy(f32[32,256,128]{2,1,0:T(8,128)S(1)} %get-tuple-element.15) | data formatting | bytes 8388608

commit v3 on v2

--- a/solution.py
+++ b/solution.py
@@ -55,7 +55,7 @@
 
 def kernel(
     inv_hbm, cost_hbm, lo_hbm, hi_hbm, iface_hbm, sub_hbm, live_hbm, weight_hbm, target_hbm,
-    dual_ref, cons_ref, norm_ref, part0,
+    both_ref, norm_ref, part0,
     mat, cost, lob, hib, cols, coef,
     base0, ai, ci, li, hi_i, lcb, sd, out, ri,
     sbuf, cbuf, rep, rbuf, sdo, idbuf, idin, hot, hot_t,
@@ -66,8 +66,9 @@
     x, z, y, c = [lax.axis_index(a) for a in AXES]
     me = ((x * 4 + z) * 4 + y) * 2 + c
     k_me = x * 4 + z
-    own = (c == 1) & (y < OWNERS)
-    part = jnp.where(y < OWNERS, y, 0)
+    place = lax.rem(y - x - z + 8, 4)
+    own = (c == 1) & (place < OWNERS)
+    part = jnp.where(place < OWNERS, place, 0)
 
     def peer(dx, dz, dy, dc):
         t = (lax.rem(x + dx, 4), lax.rem(z + dz, 4), lax.rem(y + dy, 4), lax.rem(c + dc, 2))
@@ -133,7 +134,7 @@
     to_smem.start()
 
     zero8 = jnp.zeros((F, 8, C), f32)
-    for ref in (ai, ci, li, hi_i, lcb, sd):
+    for ref in (base0, ai, ci, li, hi_i, lcb, sd):
         ref[...] = zero8
     coef[...] = jnp.zeros((F, Q, 8, C), f32)
     out[F] = jnp.zeros((8, C), f32)
@@ -145,16 +146,17 @@
             tx, tz = lax.rem(x + dx, 4), lax.rem(z + dz, 4)
             k = tx * 4 + tz
             for o in (2, 1, 0):
+                ty = lax.rem(tx + tz + o, 4)
                 copy = pltpu.make_async_remote_copy(
                     source(o, k),
                     dest.at[pl.ds(first + me * 6, 6), :],
                     s_sem,
                     r_sem,
-                    device_id=(tx, tz, o, 1),
+                    device_id=(tx, tz, ty, 1),
                     device_id_type=MESH,
                 )
                 if (dx, dz) == (0, 0):
-                    pl.when(jnp.logical_not((y == o) & (c == 1)))(copy.start)
+                    pl.when(jnp.logical_not((y == ty) & (c == 1)))(copy.start)
                 else:
                     copy.start()
 
@@ -182,15 +184,14 @@
         return pick.astype(bf16), 1.0 - jnp.sum(pick, axis=0, keepdims=True)
 
     def prepare(f):
-        pick, _ = picks(f)
-        rows = mm(pick, mat[f, 0:K, :]).astype(bf16)
-        mat[f, K : K + 16, :] = rows
-        base0[f] = mm(rows, (-cost[f]).astype(bf16))[0:8]
+        part0[f] = mm(mat[f, 0:K, :], (-cost[f]).astype(bf16))
+        for q in range(Q):
+            base0[f, q : q + 1, :] = part0[f, pl.ds(iface[q, f], 1), :]
 
     def complete(f):
         pick, keep = picks(f)
         cols[f] = mm(mat[f, 0:K, :], pick, NT).astype(bf16)
-        rows = mat[f, K : K + 16, :]
+        rows = mm(pick, mat[f, 0:K, :]).astype(bf16)
         cross = mm(rows, pick, NT)
         mat[f, K : K + 16, :] = rows * keep.astype(bf16)
         for q in range(Q):
@@ -205,10 +206,8 @@
 
     def first(f):
         _, keep = picks(f)
-        inverse = mat[f, 0:K, :]
-        primal = mm(inverse, (-cost[f]).astype(bf16))
-        mat[f, 0:K, :] = inverse * keep.astype(bf16)
-        anchor = jnp.minimum(jnp.maximum(primal, lob[f]), hib[f])
+        mat[f, 0:K, :] = mat[f, 0:K, :] * keep.astype(bf16)
+        anchor = jnp.minimum(jnp.maximum(part0[f], lob[f]), hib[f])
         solve(f, (anchor - cost[f]).astype(bf16))
 
     def solve(f, base):
@@ -390,7 +389,7 @@
     lax.fori_loop(0, ITERS, lambda t, carry: exchange(t), 0)
 
     for q in range(Q):
-        dual_ref[q] = PENALTY * sd[:, q, :]
+        both_ref[q] = PENALTY * sd[:, q, :]
 
     @pl.when(own)
     def _():
@@ -404,7 +403,7 @@
 
     for o in range(OWNERS):
         for q in range(2):
-            cons_ref[2 * o + q] = consin[o, 32 * q : 32 * q + 32, :]
+            both_ref[Q + 2 * o + q] = consin[o, 32 * q : 32 * q + 32, :]
     root = jnp.sqrt(jnp.sum(resin[...], axis=0, keepdims=True))
     norm_ref[0:1, :] = root[:, 0:ITERS]
     norm_ref[1:2, :] = PENALTY * root[:, 64 : 64 + ITERS]
@@ -423,12 +422,12 @@
     anyspace = pl.BlockSpec(memory_space=pl.ANY)
     on_vmem = pl.BlockSpec(memory_space=pltpu.VMEM)
     dma = pltpu.SemaphoreType.DMA
-    shapes = ((Q, F, C), (Q, 32, C), (2, ITERS), (F, K, C))
-    duals, consensus, norms, setpoints = pl.pallas_call(
+    shapes = ((2 * Q, F, C), (2, ITERS), (F, K, C))
+    both, norms, setpoints = pl.pallas_call(
         kernel,
         out_shape=tuple(vmem(shape) for shape in shapes),
         in_specs=[anyspace] * 9,
-        out_specs=(on_vmem,) * 4,
+        out_specs=(on_vmem,) * 3,
         scratch_shapes=[
             pltpu.VMEM((F, K + 16, K), bf16),
             vmem((F, K, C)),
@@ -490,6 +489,7 @@
             collective_id=0, has_side_effects=True, vmem_limit_bytes=58 * 2**20
         ),
     )(*operands)
+    duals, consensus = both[:Q], both[Q:]
     return duals.transpose(1, 0, 2), consensus.transpose(1, 0, 2), norms.T, setpoints
 
 

time: 83.4 us -> 79.7 us (0.956)
  Pallas kernels: 78.2 us -> 75 us
    pallas_call x1, Pallas kernels: 78.2 us -> 75 us  [shards(): pl.pallas_call(kernel, out_shape=tuple((vmem(shape) for shape in shapes))...]
    unnamed x4 -> x2, local copies, waits for them, and re-layouts: 3.86 us -> 2.58 us
where the time goes in v3:
time: 79.7 us; the launch traced here: 79.6 us
  Pallas kernels  75 us (94%)
  local copies, waits for them, and re-layouts  3.26 us (4%)
  between operations  1.29 us (2%)
    pallas_call x1, Pallas kernels, shards(): pl.pallas_call(kernel, out_shape=tuple((vmem(shape) for shape in shapes))...  75 us
    unnamed x2, local copies, waits for them, and re-layouts  2.58 us

profile of v3, /device:TPU:1, one launch (start us, length us, event | category | flops | bytes accessed | tf_op | source)
XLA Modules:
  0.0 79.6 jit_solution(896451066806830988)
XLA Ops:
  1.3 75.0 %shard_map.120 = (f32[12,32,128]{2,1,0:T(8,128)S(1)}, f32[2,5]{1,0:T(2,128)S(1)}, f32[32,256,128]{2,1,0:T(8,128)S(1)}) custom-call(bf16[32,256,256]{2,1,0:T(8,128)(2,1)} %inv_hbm.1, f32[32,256,128]{2,1,0:T(8,128)} %cost_hbm.1, f32[32,256]{1,0:T(8,128)} %lo_hbm.1, f32[32,256]{1,0:T(8,128)} %hi_hbm.1, s32[6,32]{1,0:T(8,128)} %bitcast.9, s32[32]{0:T(128)} %sub_hbm.1, ...), custom_call_target="tpu_custom_call" | custom-call | tf_op jit(solution)/shard_map/pallas_call | solution.py:426
  76.3 0.6 copy.15
  76.9 0.7 slice_bitcast_fusion
  77.6 2.0 %copy.16 = f32[32,256,128]{2,1,0:T(8,128)} copy(f32[32,256,128]{2,1,0:T(8,128)S(1)} %get-tuple-element.15) | data formatting | bytes 8388608

commit v4 on v3

--- a/solution.py
+++ b/solution.py
@@ -341,6 +341,20 @@
                 ).start()
             for i in range(6):
                 rbuf[pl.ds(part * 96 + k_me * 6 + i, 1), :] = rep[pl.ds(me * 6 + i, 1), :]
+
+            @pl.when(t == ITERS - 1)
+            def _():
+                for d in ALL:
+                    if d[:2] == (0, 0):
+                        pltpu.make_async_remote_copy(
+                            rows_new,
+                            consin.at[part],
+                            k_s,
+                            k_r,
+                            device_id=peer(*d)[0],
+                            device_id_type=MESH,
+                        ).start()
+
             next_sd = arrived[...] - rep[...]
             miss = next_sd - sdo[...]
             sdo[...] = next_sd
@@ -355,10 +369,6 @@
             def _():
                 for dx, dz, dy, dc in ALL:
                     to, number = peer(dx, dz, dy, dc)
-                    if (dx, dz) == (0, 0):
-                        pltpu.make_async_remote_copy(
-                            rows_new, consin.at[part], k_s, k_r, device_id=to, device_id_type=MESH
-                        ).start()
                     pltpu.make_async_remote_copy(
                         res, resin.at[pl.ds(part * 16 + k_me, 1), :], n_s, n_r, device_id=to, device_id_type=MESH
                     ).start()

time: 79.7 us -> 79.8 us (level)
  no operation moved by 1% of the time
where the time goes in v4:
time: 79.8 us; the launch traced here: 79.7 us
  Pallas kernels  75.1 us (94%)
  local copies, waits for them, and re-layouts  3.26 us (4%)
  between operations  1.29 us (2%)
    pallas_call x1, Pallas kernels, shards(): pl.pallas_call(kernel, out_shape=tuple((vmem(shape) for shape in shapes))...  75.1 us
    unnamed x2, local copies, waits for them, and re-layouts  2.58 us

profile of v4, /device:TPU:1, one launch (start us, length us, event | category | flops | bytes accessed | tf_op | source)
XLA Modules:
  0.0 79.7 jit_solution(14409295550117301712)
XLA Ops:
  1.3 75.1 %shard_map.120 = (f32[12,32,128]{2,1,0:T(8,128)S(1)}, f32[2,5]{1,0:T(2,128)S(1)}, f32[32,256,128]{2,1,0:T(8,128)S(1)}) custom-call(bf16[32,256,256]{2,1,0:T(8,128)(2,1)} %inv_hbm.1, f32[32,256,128]{2,1,0:T(8,128)} %cost_hbm.1, f32[32,256]{1,0:T(8,128)} %lo_hbm.1, f32[32,256]{1,0:T(8,128)} %hi_hbm.1, s32[6,32]{1,0:T(8,128)} %bitcast.9, s32[32]{0:T(128)} %sub_hbm.1, ...), custom_call_target="tpu_custom_call" | custom-call | tf_op jit(solution)/shard_map/pallas_call | solution.py:436
  76.4 0.6 copy.15
  77.0 0.7 slice_bitcast_fusion
  77.7 2.0 %copy.16 = f32[32,256,128]{2,1,0:T(8,128)} copy(f32[32,256,128]{2,1,0:T(8,128)S(1)} %get-tuple-element.15) | data formatting | bytes 8388608
